TPU v7x, 32 devices: a whole 2x2x4 slice. The times are simulated.
32 devices in a mesh: gx: 4 (over y, x), gy: 2 (over core), gz: 4 (over z).
Axes of the slice: x: 2, y: 2, z: 4, core: 2. Of those that a mesh axis runs over, the one named last changes fastest.
Arguments:
- pair: bfloat16 [128, 1024, 1024], P('gz', 'gy', 'gx'), may hold values from -6 to 6
- pair_mask: int32 [1024, 1024], P('gy', 'gx'), may hold values 0 or 1
- in_gain: float32 [128], replicated, may hold values from 0.5 to 2
- w_left: bfloat16 [128, 128], P(None, 'gz'), may hold values from -0.5 to 0.5
- w_left_gate: bfloat16 [128, 128], P(None, 'gz'), may hold values from -0.5 to 0.5
- w_right: bfloat16 [128, 128], P(None, 'gz'), may hold values from -0.5 to 0.5
- w_right_gate: bfloat16 [128, 128], P(None, 'gz'), may hold values from -0.5 to 0.5
- w_out_gate: bfloat16 [128, 128], P(None, 'gz'), may hold values from -0.5 to 0.5
- out_gain: float32 [128], P('gz'), may hold values from 0.5 to 2
- w_out: bfloat16 [128, 128], P(None, 'gz'), may hold values from -0.5 to 0.5
Outputs:
- update: bfloat16 [128, 1024, 1024], P('gz', 'gy', 'gx')
All inputs are finite; a program needn't handle non-finite values. No bound on the sum of `pair_mask` on one device may be relied on, other than what follows from the above.
Results may differ from a plain program's by a relative error of at most 0.0078.
Values may be sent and summed in bfloat16 or wider, within the bound.
No kernel may reach another device: no remote copies, remote signals or barrier semaphores. Data moves between devices by JAX's collectives and lax.ppermute only.
A program may use at most 192 MiB of HBM per device.

v0:
```python
import jax
import jax.numpy as jnp
from jax import lax
from jax.sharding import PartitionSpec as P

epsilon = 1e-05


def local(
    pair,
    pair_mask,
    in_gain,
    w_left,
    w_left_gate,
    w_right,
    w_right_gate,
    w_out_gate,
    out_gain,
    w_out,
):
    gathered = lax.all_gather(pair, "gz", axis=0, tiled=True).astype(jnp.float32)
    average = jnp.mean(gathered, axis=0)
    centered = gathered - average
    spread = jnp.mean(jnp.square(centered), axis=0)
    normed = (centered * lax.rsqrt(spread + epsilon) * in_gain[:, None, None]).astype(jnp.bfloat16)
    mask_float = pair_mask.astype(jnp.float32)[None]

    def project(weight):
        return jnp.einsum("cik,ch->hik", normed, weight, preferred_element_type=jnp.float32)

    left_rows = (mask_float * jax.nn.sigmoid(project(w_left_gate)) * project(w_left)).astype(
        jnp.bfloat16
    )
    right_rows = (mask_float * jax.nn.sigmoid(project(w_right_gate)) * project(w_right)).astype(
        jnp.bfloat16
    )
    out_gate = jax.nn.sigmoid(
        jnp.einsum("cij,cd->dij", normed, w_out_gate, preferred_element_type=jnp.float32)
    )
    left_group, right_group = (
        lax.all_to_all(left_rows, "gx", split_axis=0, concat_axis=2, tiled=True),
        lax.all_to_all(right_rows, "gx", split_axis=0, concat_axis=2, tiled=True),
    )
    full_product = lax.dot_general(
        left_group,
        lax.all_gather(right_group, "gy", axis=1, tiled=True),
        (((2,), (2,)), ((0,), (0,))),
        preferred_element_type=jnp.float32,
    )
    mixed_sum = lax.all_to_all(full_product, "gx", split_axis=2, concat_axis=0, tiled=True)
    channel_count = lax.axis_size("gz") * mixed_sum.shape[0]
    sum_terms = lax.psum(jnp.sum(mixed_sum, axis=0), "gz")
    mix_average = sum_terms / channel_count
    mix_centered = mixed_sum - mix_average
    mix_spread = lax.psum(jnp.sum(jnp.square(mix_centered), axis=0), "gz") / channel_count
    local_mix = (mix_centered * lax.rsqrt(mix_spread + epsilon) * out_gain[:, None, None]).astype(
        jnp.bfloat16
    )
    normed_mix = lax.all_gather(local_mix, "gz", axis=0, tiled=True)
    projected = jnp.einsum("hij,hd->dij", normed_mix, w_out, preferred_element_type=jnp.float32)
    return (out_gate * projected).astype(jnp.bfloat16)


def solution(mesh):
    placed = (
        P("gz", "gy", "gx"),
        P("gy", "gx"),
        P(),
        P(None, "gz"),
        P(None, "gz"),
        P(None, "gz"),
        P(None, "gz"),
        P(None, "gz"),
        P("gz"),
        P(None, "gz"),
    )
    return jax.shard_map(
        local, mesh=mesh, in_specs=placed, out_specs=P("gz", "gy", "gx"), check_vma=False
    )
```

profile of v0, /device:TPU:0, one launch (start us, length us, event | category | flops | bytes accessed | tf_op | source)
XLA Modules:
  0.0 1984.1 jit_solution(8913950968688597543)
XLA Ops:
  8.4 564.6 %all-gather.4.cloned.1.call-done = bf16[128,512,256]{2,1,0:T(8,128)(2,1)} async-done(((bf16[32,512,256]{2,1,0:T(8,128)(2,1)}), bf16[128,512,256]{2,1,0:T(8,128)(2,1)}) %all-gather.4.cloned.1.call-update) | async-done | bytes 33554448 | tf_op jit(solution)/shard_map/all_gather | solution.py:21
  573.0 11.4 convert_reduce_fusion
  584.5 11.7 fusion.2
  596.2 23.0 %fusion.4 = bf16[128,512,256]{2,1,0:T(8,128)(2,1)} fusion(bf16[128,512,256]{2,1,0:T(8,128)(2,1)} %all-gather.4.cloned.1.call-done, f32[128]{0:T(128)S(1)} %copy-done.4, f32[512,256]{1,0:T(8,128)S(1)} %add_rsqrt_fusion.1, f32[512,256]{1,0:T(8,128)S(1)} %broadcast_multiply_fusion.1), kind=kLoop, calls=%fused_computation.6 | loop fusion | flops 83886080 | bytes 68157952 | tf_op jit(solution)/shard_map/convert_element_type | solution.py:25
  619.3 35.7 %fusion.11 = f32[512,256,32]{1,2,0:T(8,128)} fusion(bf16[128,512,256]{2,1,0:T(8,128)(2,1)} %fusion.4, bf16[128,32]{0,1:T(8,128)(2,1)S(1)} %copy-done), kind=kOutput, calls=%fused_computation.13 | convolution fusion | flops 1073741824 | bytes 50339840 | tf_op jit(solution)/shard_map/cik,ch->hik/dot_general | solution.py:29
  655.0 38.1 %fusion.28 = bf16[32,512,256]{2,0,1:T(8,128)(2,1)} fusion(bf16[128,512,256]{2,1,0:T(8,128)(2,1)} %fusion.4, f32[512,256,32]{1,2,0:T(8,128)} %fusion.11, f32[512,256]{1,0:T(8,128)S(1)} %convert_element_type.23, bf16[128,32]{0,1:T(8,128)(2,1)S(1)} %copy-done.6), kind=kOutput, calls=%fused_computation.32 | convolution fusion | flops 1098907648 | bytes 59252736 | tf_op jit(solution)/shard_map/cik,ch->hik/dot_general | solution.py:29
  704.5 97.4 %all_to_all.54 = bf16[32,512,256]{2,1,0:T(8,128)(2,1)S(1)} all-to-all(bf16[32,512,256]{2,1,0:T(8,128)(2,1)} %copy.27), channel_id=1, replica_groups=mesh['gx'=4,'gy'=2,'gz'=4] {'gx'}, dimensions={0} | all-to-all | bytes 16777216 | tf_op jit(solution)/shard_map/all_to_all | solution.py:42
  809.1 14.3 all_to_all.46
  823.5 37.6 %fusion.7 = f32[512,256,32]{1,2,0:T(8,128)} fusion(bf16[128,512,256]{2,1,0:T(8,128)(2,1)} %fusion.4, bf16[128,32]{0,1:T(8,128)(2,1)S(1)} %copy-done.2), kind=kOutput, calls=%fused_computation.9 | convolution fusion | flops 1073741824 | bytes 50339840 | tf_op jit(solution)/shard_map/cik,ch->hik/dot_general | solution.py:29
  861.2 38.1 %fusion.25 = bf16[32,512,256]{2,0,1:T(8,128)(2,1)} fusion(bf16[128,512,256]{2,1,0:T(8,128)(2,1)} %fusion.4, f32[512,256,32]{1,2,0:T(8,128)} %fusion.7, f32[512,256]{1,0:T(8,128)S(1)} %convert_element_type.23, bf16[128,32]{0,1:T(8,128)(2,1)S(1)} %copy-done.7), kind=kOutput, calls=%fused_computation.31 | convolution fusion | flops 1098907648 | bytes 59252736 | tf_op jit(solution)/shard_map/cik,ch->hik/dot_general | solution.py:29
  899.3 11.4 copy.23
  910.7 94.8 %all_to_all.55 = bf16[32,512,256]{2,1,0:T(8,128)(2,1)S(1)} all-to-all(bf16[32,512,256]{2,1,0:T(8,128)(2,1)} %copy.23), channel_id=1, replica_groups=mesh['gx'=4,'gy'=2,'gz'=4] {'gx'}, dimensions={0} | all-to-all | bytes 16777216 | tf_op jit(solution)/shard_map/all_to_all | solution.py:41
  1012.8 14.3 all_to_all.42
  1027.1 17.0 fusion.37
  1044.0 17.6 copy.29
  1061.6 190.6 %all_to_all.56 = f32[8,512,1024]{1,0,2:T(8,128)} all-to-all(f32[8,512,1024]{1,0,2:T(8,128)} %copy.29), channel_id=1, replica_groups=mesh['gx'=4,'gy'=2,'gz'=4] {'gx'}, dimensions={2} | all-to-all | bytes 33554432 | tf_op jit(solution)/shard_map/all_to_all | solution.py:50
  1252.3 20.2 %copy.30 = f32[8,512,4,256]{3,0,2,1:T(8,128)} copy(f32[8,512,4,256]{1,0,3,2:T(8,128)} %bitcast.52) | data formatting | bytes 33554432 | tf_op jit(solution)/shard_map/all_to_all | solution.py:50
  1282.1 36.2 %all-reduce.3.cloned.1.call-done = f32[512,256]{1,0:T(8,128)} async-done(((f32[512,256]{1,0:T(8,128)}), f32[512,256]{1,0:T(8,128)}) %all-reduce.3.cloned.1.call-update) | async-done | bytes 524304 | tf_op jit(solution)/shard_map/psum | solution.py:52
  1319.3 12.2 fusion.19
  1331.6 38.6 %all-reduce.5.cloned.1.call-done = f32[512,256]{1,0:T(8,128)} async-done(((f32[512,256]{1,0:T(8,128)}), f32[512,256]{1,0:T(8,128)}) %all-reduce.5.cloned.1.call-update) | async-done | bytes 524304 | tf_op jit(solution)/shard_map/psum | solution.py:55
  1382.4 35.8 %fusion.5 = f32[512,256,32]{1,2,0:T(8,128)} fusion(bf16[128,512,256]{2,1,0:T(8,128)(2,1)} %fusion.4, bf16[128,32]{0,1:T(8,128)(2,1)S(1)} %copy-done.3), kind=kOutput, calls=%fused_computation.7 | convolution fusion | flops 1073741824 | bytes 50339840 | tf_op jit(solution)/shard_map/cij,cd->dij/dot_general | solution.py:38
  1418.2 525.5 %all-gather.8.cloned.1.call-done = bf16[128,512,256]{2,0,1:T(8,128)(2,1)} async-done(((bf16[32,512,256]{2,0,1:T(8,128)(2,1)}), bf16[128,512,256]{2,0,1:T(8,128)(2,1)}) %all-gather.8.cloned.1.call-update) | async-done | bytes 33554448 | tf_op jit(solution)/shard_map/all_gather | solution.py:59
  1943.8 21.8 %fusion.24 = bf16[32,512,256]{2,0,1:T(8,128)(2,1)} fusion(bf16[128,512,256]{2,0,1:T(8,128)(2,1)} %all-gather.8.cloned.1.call-done, f32[512,256,32]{1,2,0:T(8,128)} %fusion.5, bf16[128,32]{0,1:T(8,128)(2,1)S(1)} %copy-done.8), kind=kOutput, calls=%fused_computation.30 | convolution fusion | flops 1094713344 | bytes 58728448 | tf_op jit(solution)/shard_map/hij,hd->dij/dot_general | solution.py:60
  1965.6 11.5 copy.31
  (39 shorter events, 50.9 us)
Async XLA Ops:
  6.5 612.8 %copy-start = (bf16[128,32]{0,1:T(8,128)(2,1)S(1)}, bf16[128,32]{0,1:T(8,128)(2,1)}, u32[]{:S(2)}) copy-start(bf16[128,32]{0,1:T(8,128)(2,1)} %param.16) | copy-start | bytes 24580
  6.5 566.5 %all-gather.4.cloned.1.call-start = ((), (), s32[]{:S(2)}) async-start(), calls=%async_computation.3 | async-start | bytes 41943040 | tf_op jit(solution)/shard_map/all_gather | solution.py:21
  7.3 1019.8 %all-gather.6.cloned.1.call-start = ((), (), s32[]{:S(2)}) async-start(), calls=%async_computation.4 | async-start | bytes 25165824 | tf_op jit(solution)/shard_map/all_gather | solution.py:46
  584.5 11.8 copy-start.4
  619.3 35.7 %copy-start.6 = (bf16[128,32]{0,1:T(8,128)(2,1)S(1)}, bf16[128,32]{0,1:T(8,128)(2,1)}, u32[]{:S(2)}) copy-start(bf16[128,32]{0,1:T(8,128)(2,1)} %param.15) | copy-start | bytes 24580
  809.1 14.4 copy-start.2
  823.5 37.7 %copy-start.7 = (bf16[128,32]{0,1:T(8,128)(2,1)S(1)}, bf16[128,32]{0,1:T(8,128)(2,1)}, u32[]{:S(2)}) copy-start(bf16[128,32]{0,1:T(8,128)(2,1)} %param.13) | copy-start | bytes 24580
  823.5 494.7 %all-reduce.3.cloned.1.call-start = ((), (), s32[]{:S(2)}) async-start(), calls=%async_computation.5 | async-start | bytes 1048576 | tf_op jit(solution)/shard_map/psum | solution.py:52
  1272.5 98.7 %copy-start.5 = (f32[32]{0:T(128)S(1)}, f32[32]{0:T(128)}, u32[]{:S(2)}) copy-start(f32[32]{0:T(128)} %param.18) | copy-start | bytes 388
  1282.0 88.1 %all-reduce.5.cloned.1.call-start = ((), (), s32[]{:S(2)}) async-start(), calls=%async_computation.6 | async-start | bytes 1048576 | tf_op jit(solution)/shard_map/psum | solution.py:55
  1331.5 612.2 %all-gather.8.cloned.1.call-start = ((), (), s32[]{:S(2)}) async-start(), calls=%async_computation.7 | async-start | bytes 41943040 | tf_op jit(solution)/shard_map/all_gather | solution.py:59
  1371.3 11.1 copy-start.3
  1382.4 561.3 %copy-start.8 = (bf16[128,32]{0,1:T(8,128)(2,1)S(1)}, bf16[128,32]{0,1:T(8,128)(2,1)}, u32[]{:S(2)}) copy-start(bf16[128,32]{0,1:T(8,128)(2,1)} %param.19) | copy-start | bytes 24580
  1943.7 33.4 %copy-start.1 = (bf16[128,32]{0,1:T(8,128)(2,1)S(1)}, bf16[128,32]{0,1:T(8,128)(2,1)}, u32[]{:S(2)}) copy-start(bf16[128,32]{0,1:T(8,128)(2,1)} %param.16) | copy-start | bytes 24580
Sparse Core Ops, SparseCore 0:
  8.9 564.0 all-gather.3
  823.6 26.7 all-gather.5
  1282.1 36.0 all-reduce.2
  1331.6 38.4 all-reduce.4
  1382.5 561.1 all-gather.7
where the time goes:
time: 1990 us; the launch traced here: 1980 us
  waiting for transfers between devices  1170 us (59%)
  blocking collectives  383 us (19%)
  matrix products  224 us (11%)
  local copies, waits for them, and re-layouts  115 us (6%)
  other arithmetic  82.3 us (4%)
    all_gather x1, waiting for transfers between devices, local(): lax.all_gather(pair, 'gz', axis=0, tiled=True).astype(jnp.float32)  565 us
    all_gather x1, waiting for transfers between devices, local(): normed_mix = lax.all_gather(local_mix, 'gz', axis=0, tiled=True)  526 us
    all_to_all x1, blocking collectives, local(): lax.all_to_all(full_product, 'gx', split_axis=2, concat_axis=0, tiled=True)  191 us
    dot_general x4, matrix products, project(): jnp.einsum('cik,ch->hik', normed, weight, preferred_element_type=jnp.floa...  150 us
    all_to_all x1, blocking collectives, local(): lax.all_to_all(right_rows, 'gx', split_axis=0, concat_axis=2, tiled=True)  97.4 us
    all_to_all x1, blocking collectives, local(): lax.all_to_all(left_rows, 'gx', split_axis=0, concat_axis=2, tiled=True)  94.8 us
  transfers between devices with their start and end apart: 5, of which 4 were waited for; matrix products, arithmetic and copies ran while one was open for 7% of the time, Pallas kernels for 0%

commit v1 on v0

--- a/solution.py
+++ b/solution.py
@@ -56,7 +56,12 @@
     local_mix = (mix_centered * lax.rsqrt(mix_spread + epsilon) * out_gain[:, None, None]).astype(
         jnp.bfloat16
     )
-    normed_mix = lax.all_gather(local_mix, "gz", axis=0, tiled=True)
+    ring = [local_mix]
+    for hop in range(3):
+        ring.append(lax.ppermute(ring[-1], "gz", [(dev, (dev + 1) % 4) for dev in range(4)]))
+    normed_mix = jnp.roll(
+        jnp.concatenate(ring[::-1], axis=0), (lax.axis_index("gz") + 1) * ring[0].shape[0], axis=0
+    )
     projected = jnp.einsum("hij,hd->dij", normed_mix, w_out, preferred_element_type=jnp.float32)
     return (out_gate * projected).astype(jnp.bfloat16)
 

time: 1990 us -> 2050 us (1.030)
  local copies, waits for them, and re-layouts: 115 us -> 164 us
    all_gather x1 -> x0, waiting for transfers between devices: 526 us -> none  [local(): normed_mix = lax.all_gather(local_mix, 'gz', axis=0, tiled=True)]
    ppermute x0 -> x3, waiting for transfers between devices: none -> 509 us  [local(): lax.ppermute(ring[-1], 'gz', [(dev, (dev + 1) % 4) for dev in range(4)])]
    unnamed x18 -> x26, local copies, waits for them, and re-layouts: 0.05 us -> 48.8 us
  transfers between devices with their start and end apart: 5 -> 7, of which waited for: 4 -> 6; matrix products, arithmetic and copies ran while one was open for 7% -> 6% of each run, Pallas kernels for 0% -> 0%
where the time goes in v1:
time: 2050 us; the launch traced here: 2040 us
  waiting for transfers between devices  1150 us (56%)
  blocking collectives  383 us (19%)
  matrix products  225 us (11%)
  local copies, waits for them, and re-layouts  164 us (8%)
  other arithmetic  102 us (5%)
    all_gather x1, waiting for transfers between devices, local(): lax.all_gather(pair, 'gz', axis=0, tiled=True).astype(jnp.float32)  565 us
    ppermute x3, waiting for transfers between devices, local(): lax.ppermute(ring[-1], 'gz', [(dev, (dev + 1) % 4) for dev in range(4)])  509 us
    all_to_all x1, blocking collectives, local(): lax.all_to_all(full_product, 'gx', split_axis=2, concat_axis=0, tiled=True)  191 us
    dot_general x4, matrix products, project(): jnp.einsum('cik,ch->hik', normed, weight, preferred_element_type=jnp.floa...  149 us
    all_to_all x1, blocking collectives, local(): lax.all_to_all(right_rows, 'gx', split_axis=0, concat_axis=2, tiled=True)  97.4 us
    all_to_all x1, blocking collectives, local(): lax.all_to_all(left_rows, 'gx', split_axis=0, concat_axis=2, tiled=True)  94.8 us
    unnamed x26, local copies, waits for them, and re-layouts  48.8 us
  transfers between devices with their start and end apart: 7, of which 6 were waited for; matrix products, arithmetic and copies ran while one was open for 6% of the time, Pallas kernels for 0%

profile of v1, /device:TPU:0, one launch (start us, length us, event | category | flops | bytes accessed | tf_op | source)
XLA Modules:
  0.0 2038.4 jit_solution(6437507996356797742)
XLA Ops:
  8.4 564.6 %all-gather.3.cloned.1.call-done = bf16[128,512,256]{2,1,0:T(8,128)(2,1)} async-done(((bf16[32,512,256]{2,1,0:T(8,128)(2,1)}), bf16[128,512,256]{2,1,0:T(8,128)(2,1)}) %all-gather.3.cloned.1.call-update) | async-done | bytes 33554448 | tf_op jit(solution)/shard_map/all_gather | solution.py:21
  584.5 11.7 fusion.2
  596.2 23.0 %fusion.4 = bf16[128,512,256]{2,1,0:T(8,128)(2,1)} fusion(bf16[128,512,256]{2,1,0:T(8,128)(2,1)} %all-gather.3.cloned.1.call-done, f32[128]{0:T(128)S(1)} %copy-done.6, f32[512,256]{1,0:T(8,128)S(1)} %add_rsqrt_fusion.1, f32[512,256]{1,0:T(8,128)S(1)} %broadcast_multiply_fusion.1), kind=kLoop, calls=%fused_computation.6 | loop fusion | flops 83886080 | bytes 68157952 | tf_op jit(solution)/shard_map/convert_element_type | solution.py:25
  619.2 35.7 %fusion.13 = f32[512,256,32]{1,2,0:T(8,128)} fusion(bf16[128,512,256]{2,1,0:T(8,128)(2,1)} %fusion.4, bf16[128,32]{0,1:T(8,128)(2,1)S(1)} %copy-done), kind=kOutput, calls=%fused_computation.15 | convolution fusion | flops 1073741824 | bytes 50339840 | tf_op jit(solution)/shard_map/cik,ch->hik/dot_general | solution.py:29
  654.9 38.1 %fusion.34 = bf16[32,512,256]{2,0,1:T(8,128)(2,1)} fusion(bf16[128,512,256]{2,1,0:T(8,128)(2,1)} %fusion.4, f32[512,256,32]{1,2,0:T(8,128)} %fusion.13, f32[512,256]{1,0:T(8,128)S(1)} %convert_element_type.23, bf16[128,32]{0,1:T(8,128)(2,1)S(1)} %copy-done.7), kind=kOutput, calls=%fused_computation.34 | convolution fusion | flops 1098907648 | bytes 59252736 | tf_op jit(solution)/shard_map/cik,ch->hik/dot_general | solution.py:29
  704.4 97.4 %all_to_all.54 = bf16[32,512,256]{2,1,0:T(8,128)(2,1)S(1)} all-to-all(bf16[32,512,256]{2,1,0:T(8,128)(2,1)} %copy.27), channel_id=1, replica_groups=mesh['gx'=4,'gy'=2,'gz'=4] {'gx'}, dimensions={0} | all-to-all | bytes 16777216 | tf_op jit(solution)/shard_map/all_to_all | solution.py:42
  809.0 14.3 all_to_all.46
  823.4 37.6 %fusion.9 = f32[512,256,32]{1,2,0:T(8,128)} fusion(bf16[128,512,256]{2,1,0:T(8,128)(2,1)} %fusion.4, bf16[128,32]{0,1:T(8,128)(2,1)S(1)} %copy-done.3), kind=kOutput, calls=%fused_computation.11 | convolution fusion | flops 1073741824 | bytes 50339840 | tf_op jit(solution)/shard_map/cik,ch->hik/dot_general | solution.py:29
  861.0 38.1 %fusion.31 = bf16[32,512,256]{2,0,1:T(8,128)(2,1)} fusion(bf16[128,512,256]{2,1,0:T(8,128)(2,1)} %fusion.4, f32[512,256,32]{1,2,0:T(8,128)} %fusion.9, f32[512,256]{1,0:T(8,128)S(1)} %convert_element_type.23, bf16[128,32]{0,1:T(8,128)(2,1)S(1)} %copy-done.8), kind=kOutput, calls=%fused_computation.33 | convolution fusion | flops 1098907648 | bytes 59252736 | tf_op jit(solution)/shard_map/cik,ch->hik/dot_general | solution.py:29
  910.5 94.8 %all_to_all.55 = bf16[32,512,256]{2,1,0:T(8,128)(2,1)S(1)} all-to-all(bf16[32,512,256]{2,1,0:T(8,128)(2,1)} %copy.23), channel_id=1, replica_groups=mesh['gx'=4,'gy'=2,'gz'=4] {'gx'}, dimensions={0} | all-to-all | bytes 16777216 | tf_op jit(solution)/shard_map/all_to_all | solution.py:41
  1012.6 14.3 all_to_all.42
  1027.0 17.0 fusion.44
  1043.9 17.6 copy.29
  1061.5 190.6 %all_to_all.56 = f32[8,512,1024]{1,0,2:T(8,128)} all-to-all(f32[8,512,1024]{1,0,2:T(8,128)} %copy.29), channel_id=1, replica_groups=mesh['gx'=4,'gy'=2,'gz'=4] {'gx'}, dimensions={2} | all-to-all | bytes 33554432 | tf_op jit(solution)/shard_map/all_to_all | solution.py:50
  1252.1 20.2 copy.30
  1281.9 36.0 %all-reduce.3.cloned.1.call-done = f32[512,256]{1,0:T(8,128)} async-done(((f32[512,256]{1,0:T(8,128)}), f32[512,256]{1,0:T(8,128)}) %all-reduce.3.cloned.1.call-update) | async-done | bytes 524304 | tf_op jit(solution)/shard_map/psum | solution.py:52
  1318.9 12.2 fusion.21
  1331.2 38.6 %all-reduce.5.cloned.1.call-done = f32[512,256]{1,0:T(8,128)} async-done(((f32[512,256]{1,0:T(8,128)}), f32[512,256]{1,0:T(8,128)}) %all-reduce.5.cloned.1.call-update) | async-done | bytes 524304 | tf_op jit(solution)/shard_map/psum | solution.py:55
  1381.2 181.5 %collective-permute-done = bf16[32,512,256]{2,0,1:T(8,128)(2,1)S(1)} collective-permute-done((bf16[32,512,256]{2,0,1:T(8,128)(2,1)S(1)}, bf16[32,512,256]{2,0,1:T(8,128)(2,1)S(1)}, u32[]{:S(2)}, u32[]{:S(2)}) %collective-permute-start) | collective-permute-done | bytes 8388640 | tf_op jit(solution)/shard_map/ppermute | solution.py:61
  1566.1 182.3 %collective-permute-done.1 = bf16[32,512,256]{2,0,1:T(8,128)(2,1)} collective-permute-done((bf16[32,512,256]{2,0,1:T(8,128)(2,1)S(1)}, bf16[32,512,256]{2,0,1:T(8,128)(2,1)}, u32[]{:S(2)}, u32[]{:S(2)}) %collective-permute-start.1) | collective-permute-done | bytes 8388640 | tf_op jit(solution)/shard_map/ppermute | solution.py:61
  1748.5 36.2 %fusion.7 = f32[512,256,32]{1,2,0:T(8,128)} fusion(bf16[128,512,256]{2,1,0:T(8,128)(2,1)} %fusion.4, bf16[128,32]{0,1:T(8,128)(2,1)S(1)} %copy-done.4), kind=kOutput, calls=%fused_computation.9 | convolution fusion | flops 1073741824 | bytes 50339840 | tf_op jit(solution)/shard_map/cij,cd->dij/dot_general | solution.py:38
  1784.7 145.4 %collective-permute-done.2 = bf16[32,512,256]{2,0,1:T(8,128)(2,1)} collective-permute-done((bf16[32,512,256]{2,0,1:T(8,128)(2,1)}, bf16[32,512,256]{2,0,1:T(8,128)(2,1)}, u32[]{:S(2)}, u32[]{:S(2)}) %collective-permute-start.2) | collective-permute-done | bytes 8388640 | tf_op jit(solution)/shard_map/ppermute | solution.py:61
  1997.9 21.9 %fusion.28 = bf16[32,512,256]{2,0,1:T(8,128)(2,1)} fusion(bf16[256,512,256]{2,0,1:T(8,128)(2,1)} %constant_dynamic-update-slice_fusion, s32[]{:T(128)S(6)} %select_n.14, f32[512,256,32]{1,2,0:T(8,128)} %fusion.7, bf16[128,32]{0,1:T(8,128)(2,1)S(1)} %copy-done.9), kind=kOutput, calls=%fused_computation.32 | convolution fusion | flops 1094713344 | bytes 58728452 | tf_op jit(solution)/shard_map/hij,hd->dij/dot_general | solution.py:65
  2019.8 11.5 copy.31
  (52 shorter events, 143.9 us)
Async XLA Ops:
  6.5 612.7 %copy-start = (bf16[128,32]{0,1:T(8,128)(2,1)S(1)}, bf16[128,32]{0,1:T(8,128)(2,1)}, u32[]{:S(2)}) copy-start(bf16[128,32]{0,1:T(8,128)(2,1)} %param.16) | copy-start | bytes 24580
  6.5 566.5 %all-gather.3.cloned.1.call-start = ((), (), s32[]{:S(2)}) async-start(), calls=%async_computation.3 | async-start | bytes 41943040 | tf_op jit(solution)/shard_map/all_gather | solution.py:21
  7.3 1019.7 %all-gather.5.cloned.1.call-start = ((), (), s32[]{:S(2)}) async-start(), calls=%async_computation.4 | async-start | bytes 25165824 | tf_op jit(solution)/shard_map/all_gather | solution.py:46
  584.5 11.8 copy-start.6
  619.2 35.7 %copy-start.7 = (bf16[128,32]{0,1:T(8,128)(2,1)S(1)}, bf16[128,32]{0,1:T(8,128)(2,1)}, u32[]{:S(2)}) copy-start(bf16[128,32]{0,1:T(8,128)(2,1)} %param.15) | copy-start | bytes 24580
  809.0 14.4 copy-start.3
  823.4 37.7 %copy-start.8 = (bf16[128,32]{0,1:T(8,128)(2,1)S(1)}, bf16[128,32]{0,1:T(8,128)(2,1)}, u32[]{:S(2)}) copy-start(bf16[128,32]{0,1:T(8,128)(2,1)} %param.13) | copy-start | bytes 24580
  823.4 494.5 %all-reduce.3.cloned.1.call-start = ((), (), s32[]{:S(2)}) async-start(), calls=%async_computation.5 | async-start | bytes 1048576 | tf_op jit(solution)/shard_map/psum | solution.py:52
  1272.3 98.6 %copy-start.5 = (f32[32]{0:T(128)S(1)}, f32[32]{0:T(128)}, u32[]{:S(2)}) copy-start(f32[32]{0:T(128)} %param.18) | copy-start | bytes 388
  1281.8 87.9 %all-reduce.5.cloned.1.call-start = ((), (), s32[]{:S(2)}) async-start(), calls=%async_computation.6 | async-start | bytes 1048576 | tf_op jit(solution)/shard_map/psum | solution.py:55
  1331.1 417.3 %copy-start.4 = (bf16[128,32]{0,1:T(8,128)(2,1)S(1)}, bf16[128,32]{0,1:T(8,128)(2,1)}, u32[]{:S(2)}) copy-start(bf16[128,32]{0,1:T(8,128)(2,1)} %param.17) | copy-start | bytes 24580
  1379.6 183.1 %collective-permute-start = (bf16[32,512,256]{2,0,1:T(8,128)(2,1)S(1)}, bf16[32,512,256]{2,0,1:T(8,128)(2,1)S(1)}, u32[]{:S(2)}, u32[]{:S(2)}) collective-permute-start(bf16[32,512,256]{2,0,1:T(8,128)(2,1)S(1)} %fusion.19), channel_id=1, source_target_pairs={{0,1},{1,2},{2,3},{3,0},{4,5},{5,6},{6,7},{7,4},{8,9},{9,10},{10,1... | collective-permute-start | bytes 25165832 | tf_op jit(solution)/shard_map/ppermute | solution.py:61
  1562.7 3.4 copy-start.2
  1566.1 182.3 %collective-permute-start.1 = (bf16[32,512,256]{2,0,1:T(8,128)(2,1)S(1)}, bf16[32,512,256]{2,0,1:T(8,128)(2,1)}, u32[]{:S(2)}, u32[]{:S(2)}) collective-permute-start(bf16[32,512,256]{2,0,1:T(8,128)(2,1)S(1)} %collective-permute-done), channel_id=1, source_target_pairs={{0,1},{1,2},{2,3},{3,0},{4,5},{5,6},{6,7},{7,4},{8,9},{9,10},{10,1... | collective-permute-start | bytes 25165832 | tf_op jit(solution)/shard_map/ppermute | solution.py:61
  1748.5 181.7 %collective-permute-start.2 = (bf16[32,512,256]{2,0,1:T(8,128)(2,1)}, bf16[32,512,256]{2,0,1:T(8,128)(2,1)}, u32[]{:S(2)}, u32[]{:S(2)}) collective-permute-start(bf16[32,512,256]{2,0,1:T(8,128)(2,1)} %collective-permute-done.1), channel_id=1, source_target_pairs={{0,1},{1,2},{2,3},{3,0},{4,5},{5,6},{6,7},{7,4},{8,9},{9,10},{10,1... | collective-permute-start | bytes 25165832 | tf_op jit(solution)/shard_map/ppermute | solution.py:61
  1986.7 11.2 copy-start.9
  1997.9 33.5 %copy-start.1 = (bf16[128,32]{0,1:T(8,128)(2,1)S(1)}, bf16[128,32]{0,1:T(8,128)(2,1)}, u32[]{:S(2)}) copy-start(bf16[128,32]{0,1:T(8,128)(2,1)} %param.16) | copy-start | bytes 24580
Sparse Core Ops, SparseCore 0:
  8.9 564.0 all-gather.2
  823.5 26.7 all-gather.4
  1282.0 35.8 all-reduce.2
  1331.3 38.4 all-reduce.4
